TPU v7x, 32 devices: a whole 2x2x4 slice. The times are simulated.
32 devices in a mesh: expert: 4 (over x, core), tensor: 8 (over z, y).
Axes of the slice: x: 2, y: 2, z: 4, core: 2. Of those that a mesh axis runs over, the one named last changes fastest.
Arguments:
- tokens: bfloat16 [128, 7168], P('expert', 'tensor'), may hold values from -6 to 6
- routes: int32 [128, 8], P('expert'), may hold values from 0 to 15, all different within a row; in each aligned block of 128 rows (0 to 127, 128 to 255, ...) at most 128 rows name the same one
- gates: bfloat16 [128, 8], P('expert'), may hold values from 0.099609375 to 0.59765625
- w_gate: bfloat16 [16, 2048, 7168], P('expert', 'tensor'), may hold values from -0.0625 to 0.0625
- w_up: bfloat16 [16, 2048, 7168], P('expert', 'tensor'), may hold values from -0.0625 to 0.0625
- w_down: bfloat16 [16, 2048, 7168], P('expert', None, 'tensor'), may hold values from -0.125 to 0.125
Outputs:
- moe_out: bfloat16 [128, 7168], P('expert', 'tensor')
Inputs may be any that keep to these rules, and one draw needn't show every extreme that they name: `routes`: each row names 8 different experts. No expert is named by more than 128 of the 128 rows, and one expert is named by exactly 128 rows.
All inputs are finite; a program needn't handle non-finite values.
Results may differ from a plain program's by a relative error of at most 0.0049.
Values may be sent and summed in bfloat16 or wider, within the bound.
A program may use at most 128 MiB of HBM per device.

v0:
```python
import jax
import jax.numpy as jnp
from jax import lax
from jax.sharding import PartitionSpec as P

CAP = 128


def entering(value, axis, combine, identity):
    length, index = (lax.axis_size(axis), lax.axis_index(axis))
    everything = lax.all_gather(value, axis)
    start = jnp.broadcast_to(jnp.asarray(identity, value.dtype), value.shape)

    def lap(k, before):
        reached = k < index
        new = combine(before, everything[k])
        return jnp.where(reached, new, before)

    return lax.fori_loop(0, length, lap, start)


def add_counts(earlier, later):
    return earlier + later


def on_device(tokens, routes, gates, w_gate, w_up, w_down):
    exp_dev = w_gate.shape[0]
    experts = exp_dev * lax.axis_size("expert")
    group_index = lax.axis_index("expert")
    expert_ids = jnp.arange(experts, dtype=jnp.int32)
    route_hits = routes[:, :, None] == expert_ids[None, None, :]
    member = jnp.sum(route_hits.astype(jnp.int32), axis=1)
    counts = jnp.sum(member, axis=0)
    offset = entering(counts, "expert", add_counts, jnp.zeros_like(counts))
    before = jnp.cumsum(member, axis=0) - member + offset[None, :]
    own_slot = jnp.sum(jnp.where(route_hits, before[:, None, :], 0), axis=2).astype(jnp.int32)
    all_routes, all_slots = (
        lax.all_gather(routes, "expert", axis=0, tiled=True),
        lax.all_gather(own_slot, "expert", axis=0, tiled=True),
    )
    row_block, all_gates = (
        lax.all_gather(tokens, "expert", axis=0, tiled=True),
        lax.all_gather(gates, "expert", axis=0, tiled=True),
    )
    gathered = lax.all_gather(row_block, "tensor", axis=1, tiled=True)
    local_ids = all_routes - group_index * exp_dev
    is_local = (local_ids >= 0) & (local_ids < exp_dev)
    slot_id = jnp.where(is_local, local_ids * CAP + all_slots, -1)
    slot_range = jnp.arange(exp_dev * CAP, dtype=jnp.int32)
    matches = slot_id[:, :, None] == slot_range[None, None, :]
    picked = jnp.any(matches, axis=1).astype(jnp.bfloat16)
    mixing = jnp.sum(jnp.where(matches, all_gates.astype(jnp.float32)[:, :, None], 0.0), axis=1)
    slot_rows = lax.dot_general(
        picked, gathered, (((0,), (0,)), ((), ())), preferred_element_type=jnp.float32
    ).astype(jnp.bfloat16)
    slot_rows = slot_rows.reshape(exp_dev, CAP, gathered.shape[1])
    gate_proj = jnp.einsum("ecd,efd->ecf", slot_rows, w_gate, preferred_element_type=jnp.float32)
    up_proj = jnp.einsum("ecd,efd->ecf", slot_rows, w_up, preferred_element_type=jnp.float32)
    hidden = (jax.nn.silu(gate_proj) * up_proj).astype(jnp.bfloat16)
    expert_out = jnp.einsum(
        "ecf,efd->ecd",
        lax.all_gather(hidden, "tensor", axis=2, tiled=True),
        w_down,
        preferred_element_type=jnp.float32,
    )
    expert_out = expert_out.reshape(exp_dev * CAP, w_down.shape[2])
    partial_value = jnp.dot(mixing, expert_out, precision=lax.Precision.HIGHEST)
    result = lax.psum_scatter(partial_value, "expert", scatter_dimension=0, tiled=True)
    return result.astype(jnp.bfloat16)


def solution(mesh):
    placed = (
        P("expert", "tensor"),
        P("expert", None),
        P("expert", None),
        P("expert", "tensor", None),
        P("expert", "tensor", None),
        P("expert", None, "tensor"),
    )
    return jax.shard_map(
        on_device, mesh=mesh, in_specs=placed, out_specs=P("expert", "tensor"), check_vma=False
    )
```

profile of v0, /device:TPU:0, one launch (start us, length us, event | category | flops | bytes accessed | tf_op | source)
XLA Modules:
  0.0 181.3 jit_solution(15544654380891682984)
XLA Ops:
  6.5 8.7 %all_gather.29 = bf16[128,896]{1,0:T(8,128)(2,1)} all-gather(bf16[32,896]{1,0:T(8,128)(2,1)} %param.8), channel_id=1, replica_groups=mesh['expert'=4,'tensor'=8] {'expert'}, dimensions={0}, use_global_device_ids=true | all-gather | bytes 286720 | tf_op jit(solution)/shard_map/all_gather | solution.py:42
  15.3 0.0 all-gather.7.cloned.1.call-update
  15.3 0.0 all-gather.9.cloned.1.call-start
  15.3 1.2 dynamic-slice
  17.2 0.8 convert_reduce_fusion
  18.0 0.2 dynamic-update-slice
  18.2 4.3 %all-reduce = s32[64]{0:T(128)S(1)} all-reduce(s32[64]{0:T(128)S(1)} %dynamic-update-slice), channel_id=2, replica_groups=mesh['expert'=4,'tensor'=8] {'expert'}, use_global_device_ids=true, to_apply=%add | all-reduce | flops 64 | bytes 512
  22.5 0.1 reshape.32
  22.6 0.1 copy.18
  22.6 0.1 reduce_window_sum.11
  22.7 0.1 while.14
  22.9 0.1 copy.20
  22.9 0.7 select_reduce_fusion.1
  23.7 5.2 %all-gather.2 = s32[4,32,8]{1,2,0:T(8,128)S(1)} all-gather(s32[1,32,8]{1,2,0:T(8,128)S(1)} %bitcast.29), channel_id=1, replica_groups=mesh['expert'=4,'tensor'=8] {'expert'}, dimensions={0}, use_global_device_ids=true | all-gather | bytes 5120 | tf_op jit(solution)/shard_map/all_gather | solution.py:39
  28.9 5.3 %all-gather.1 = s32[4,32,8]{1,2,0:T(8,128)S(1)} all-gather(s32[1,32,8]{1,2,0:T(8,128)} %bitcast.28), channel_id=1, replica_groups=mesh['expert'=4,'tensor'=8] {'expert'}, dimensions={0}, use_global_device_ids=true | all-gather | bytes 5120 | tf_op jit(solution)/shard_map/all_gather | solution.py:38
  34.2 0.1 copy.25
  34.3 0.7 fusion
  35.0 27.3 %all-gather.7.cloned.1.call-done = bf16[128,7168]{1,0:T(8,128)(2,1)} async-done(((bf16[128,896]{1,0:T(8,128)(2,1)}), bf16[128,7168]{1,0:T(8,128)(2,1)}) %all-gather.7.cloned.1.call-update) | async-done | bytes 1835024 | tf_op jit(solution)/shard_map/all_gather | solution.py:45
  62.3 6.6 %convolution_convert_fusion = bf16[512,7168]{1,0:T(8,128)(2,1)} fusion(pred[128,512]{1,0:T(8,128)(4,1)S(1)} %fusion, bf16[128,7168]{1,0:T(8,128)(2,1)} %all-gather.7.cloned.1.call-done), kind=kOutput, calls=%fused_computation.2 | convolution fusion | flops 943194112 | bytes 9240576 | tf_op jit(solution)/shard_map/dot_general | solution.py:53
  68.9 12.3 %fusion.2 = f32[4,128,256]{2,1,0:T(8,128)S(1)} fusion(bf16[4,128,7168]{2,1,0:T(8,128)(2,1)} %bitcast.22, bf16[4,256,7168]{2,1,0:T(8,128)(2,1)} %param.11), kind=kOutput, calls=%fused_computation.14 | convolution fusion | flops 1879048192 | bytes 22544384 | tf_op jit(solution)/shard_map/ecd,efd->ecf/dot_general | solution.py:57
  81.2 13.0 %fusion.1 = bf16[4,128,256]{2,1,0:T(8,128)(2,1)} fusion(bf16[4,128,7168]{2,1,0:T(8,128)(2,1)} %bitcast.23, bf16[4,256,7168]{2,1,0:T(8,128)(2,1)} %param.12, f32[4,128,256]{2,1,0:T(8,128)S(1)} %fusion.2), kind=kOutput, calls=%fused_computation.7 | convolution fusion | flops 1879834624 | bytes 22806528 | tf_op jit(solution)/shard_map/ecd,efd->ecf/dot_general | solution.py:58
  94.2 0.0 all-gather.9.cloned.1.call-update
  94.2 0.0 reduce-scatter.2.cloned.1.call-start
  94.3 5.4 %all-gather.3 = bf16[4,32,8]{1,2,0:T(8,128)(2,1)S(1)} all-gather(bf16[1,32,8]{1,2,0:T(8,128)(2,1)S(1)} %bitcast.30), channel_id=1, replica_groups=mesh['expert'=4,'tensor'=8] {'expert'}, dimensions={0}, use_global_device_ids=true | all-gather | bytes 2560 | tf_op jit(solution)/shard_map/all_gather | solution.py:43
  99.6 0.1 copy.26
  99.7 0.7 select_reduce_fusion
  100.4 43.1 %all-gather.9.cloned.1.call-done = bf16[4,128,2048]{2,1,0:T(8,128)(2,1)} async-done(((bf16[4,128,256]{2,1,0:T(8,128)(2,1)}), bf16[4,128,2048]{2,1,0:T(8,128)(2,1)}) %all-gather.9.cloned.1.call-update) | async-done | bytes 2097168 | tf_op jit(solution)/shard_map/all_gather | solution.py:62
  143.5 8.2 %fusion.3 = f32[4,128,896]{2,1,0:T(8,128)S(1)} fusion(bf16[4,128,2048]{2,1,0:T(8,128)(2,1)} %all-gather.9.cloned.1.call-done, bf16[4,2048,896]{2,1,0:T(8,128)(2,1)} %param.13), kind=kOutput, calls=%fused_computation.15 | convolution fusion | flops 1879048192 | bytes 18612224 | tf_op jit(solution)/shard_map/ecf,efd->ecd/dot_general | solution.py:60
  151.7 2.0 %fusion.4 = f32[128,896]{1,0:T(8,128)} fusion(f32[128,512]{1,0:T(8,128)S(1)} %select_reduce_fusion, f32[512,896]{1,0:T(8,128)S(1)} %bitcast.24), kind=kOutput, calls=%fused_computation.16 | convolution fusion | flops 704643072 | bytes 2555904 | tf_op jit(solution)/shard_map/dot_general | solution.py:67
  153.7 0.0 reduce-scatter.2.cloned.1.call-update
  153.7 19.5 %reduce-scatter.2.cloned.1.call-done = f32[32,896]{1,0:T(8,128)} async-done(((f32[128,896]{1,0:T(8,128)}), f32[32,896]{1,0:T(8,128)}) %reduce-scatter.2.cloned.1.call-update) | async-done | bytes 114704 | tf_op jit(solution)/shard_map/reduce_scatter | solution.py:68
  173.2 1.5 convert_element_type.20
  (11 shorter events, 0.1 us)
Async XLA Ops:
  6.5 55.8 %all-gather.7.cloned.1.call-start = ((), (), s32[]{:S(2)}) async-start(), calls=%async_computation.1 | async-start | bytes 2064384 | tf_op jit(solution)/shard_map/all_gather | solution.py:45
  15.3 128.3 %all-gather.9.cloned.1.call-start = ((), (), s32[]{:S(2)}) async-start(), calls=%async_computation.2 | async-start | bytes 2359296 | tf_op jit(solution)/shard_map/all_gather | solution.py:62
  81.2 13.1 %copy-start = (bf16[32,8]{0,1:T(8,128)(2,1)S(1)}, bf16[32,8]{0,1:T(8,128)(2,1)}, u32[]{:S(2)}) copy-start(bf16[32,8]{0,1:T(8,128)(2,1)} %param.10) | copy-start | bytes 1540
  94.2 79.0 %reduce-scatter.2.cloned.1.call-start = ((), (), s32[]{:S(2)}) async-start(), calls=%async_computation.3 | async-start | bytes 573440 | tf_op jit(solution)/shard_map/reduce_scatter | solution.py:68
Sparse Core Ops, SparseCore 0:
  15.4 46.8 all-gather.6
  94.3 49.1 all-gather.8
  153.8 19.3 reduce-scatter.1
where the time goes:
time: 182 us; the launch traced here: 181 us
  waiting for transfers between devices  90 us (49%)
  matrix products  42 us (23%)
  blocking collectives  28.9 us (16%)
  between operations  13.8 us (8%)
  other arithmetic  4.59 us (3%)
  local copies, waits for them, and re-layouts  1.88 us (1%)
    all_gather x1, waiting for transfers between devices, on_device(): lax.all_gather(hidden, 'tensor', axis=2, tiled=True)  43.1 us
    all_gather x1, waiting for transfers between devices, on_device(): gathered = lax.all_gather(row_block, 'tensor', axis=1, tiled=True)  27.3 us
    reduce_scatter x1, waiting for transfers between devices, on_device(): lax.psum_scatter(partial_value, 'expert', scatter_dimension=0, tiled=True)  19.5 us
    dot_general x1, matrix products, on_device(): jnp.einsum('ecd,efd->ecf', slot_rows, w_up, preferred_element_type=jnp.fl...  13 us
    dot_general x1, matrix products, on_device(): jnp.einsum('ecd,efd->ecf', slot_rows, w_gate, preferred_element_type=jnp....  12.3 us
    all_gather x1, blocking collectives, on_device(): lax.all_gather(tokens, 'expert', axis=0, tiled=True)  8.71 us
    dot_general x1, matrix products, on_device(): jnp.einsum('ecf,efd->ecd', lax.all_gather(hidden, 'tensor', axis=2, tiled...  8.16 us
    dot_general x1, matrix products, on_device(): lax.dot_general(picked, gathered, (((0,), (0,)), ((), ())), preferred_ele...  6.58 us
  transfers between devices with their start and end apart: 3, of which 3 were waited for; matrix products, arithmetic and copies ran while one was open for 3% of the time, Pallas kernels for 0%

commit v1 on v0

--- a/solution.py
+++ b/solution.py
@@ -57,12 +57,38 @@
     gate_proj = jnp.einsum("ecd,efd->ecf", slot_rows, w_gate, preferred_element_type=jnp.float32)
     up_proj = jnp.einsum("ecd,efd->ecf", slot_rows, w_up, preferred_element_type=jnp.float32)
     hidden = (jax.nn.silu(gate_proj) * up_proj).astype(jnp.bfloat16)
-    expert_out = jnp.einsum(
+    size, index_2, extent = (lax.axis_size("tensor"), lax.axis_index("tensor"), hidden.shape[2])
+    upward = [(i, (i + 1) % size) for i in range(size)]
+    behind = [(i, (i - 1) % size) for i in range(size)]
+    half = size // 2
+    from_left = from_right = hidden
+    subtotal = jnp.einsum(
         "ecf,efd->ecd",
-        lax.all_gather(hidden, "tensor", axis=2, tiled=True),
-        w_down,
+        hidden,
+        lax.dynamic_slice_in_dim(w_down, index_2 * extent, hidden.shape[2], axis=1),
         preferred_element_type=jnp.float32,
     )
+    for hop in range(1, half + 1):
+        from_left = lax.ppermute(from_left, "tensor", upward)
+        if hop < size - half:
+            from_right = lax.ppermute(from_right, "tensor", behind)
+            subtotal = subtotal + jnp.einsum(
+                "ecf,efd->ecd",
+                from_right,
+                lax.dynamic_slice_in_dim(
+                    w_down, (index_2 + hop) % size * extent, from_right.shape[2], axis=1
+                ),
+                preferred_element_type=jnp.float32,
+            )
+        subtotal = subtotal + jnp.einsum(
+            "ecf,efd->ecd",
+            from_left,
+            lax.dynamic_slice_in_dim(
+                w_down, (index_2 - hop) % size * extent, from_left.shape[2], axis=1
+            ),
+            preferred_element_type=jnp.float32,
+        )
+    expert_out = subtotal
     expert_out = expert_out.reshape(exp_dev * CAP, w_down.shape[2])
     partial_value = jnp.dot(mixing, expert_out, precision=lax.Precision.HIGHEST)
     result = lax.psum_scatter(partial_value, "expert", scatter_dimension=0, tiled=True)

time: 182 us -> 175 us (0.962)
  waiting for transfers between devices: 90 us -> 66.1 us
  starting transfers between devices: 0.09 us -> 9.37 us
  matrix products: 42 us -> 49.1 us
    all_gather x1 -> x0, waiting for transfers between devices: 43.1 us -> none  [on_device(): lax.all_gather(hidden, 'tensor', axis=2, tiled=True)]
    ppermute x0 -> x7, waiting for transfers between devices: none -> 25.6 us  [the longest x3 14.7 us: on_device(): from_right = lax.ppermute(from_right, 'tensor', behind)]
    ppermute x0 -> x7, starting transfers between devices: none -> 9.33 us  [the longest x3 6 us: on_device(): from_right = lax.ppermute(from_right, 'tensor', behind)]
    dot_general x1 -> x8, matrix products: 8.16 us -> 16 us  [the longest x4 8.19 us: on_device(): jnp.einsum('ecf,efd->ecd', from_left, lax.dynamic_slice_in_dim(w_down, (i...]
    all_gather x1, waiting for transfers between devices: 27.3 us -> 21.1 us  [on_device(): gathered = lax.all_gather(row_block, 'tensor', axis=1, tiled=True)]
  transfers between devices with their start and end apart: 3 -> 9, of which waited for: 3 -> 6; matrix products, arithmetic and copies ran while one was open for 3% -> 11% of each run, Pallas kernels for 0% -> 0%
where the time goes in v1:
time: 175 us; the launch traced here: 174 us
  waiting for transfers between devices  66.1 us (38%)
  matrix products  49.1 us (28%)
  blocking collectives  28.8 us (16%)
  between operations  14.3 us (8%)
  starting transfers between devices  9.37 us (5%)
  other arithmetic  4.59 us (3%)
  local copies, waits for them, and re-layouts  1.88 us (1%)
    all_gather x1, waiting for transfers between devices, on_device(): gathered = lax.all_gather(row_block, 'tensor', axis=1, tiled=True)  21.1 us
    reduce_scatter x1, waiting for transfers between devices, on_device(): lax.psum_scatter(partial_value, 'expert', scatter_dimension=0, tiled=True)  19.4 us
    ppermute x3, waiting for transfers between devices, on_device(): from_right = lax.ppermute(from_right, 'tensor', behind)  14.7 us
    dot_general x1, matrix products, on_device(): jnp.einsum('ecd,efd->ecf', slot_rows, w_up, preferred_element_type=jnp.fl...  12.3 us
    dot_general x1, matrix products, on_device(): jnp.einsum('ecd,efd->ecf', slot_rows, w_gate, preferred_element_type=jnp....  12.3 us
    ppermute x4, waiting for transfers between devices, on_device(): from_left = lax.ppermute(from_left, 'tensor', upward)  10.9 us
    all_gather x1, blocking collectives, on_device(): lax.all_gather(tokens, 'expert', axis=0, tiled=True)  8.71 us
    dot_general x4, matrix products, on_device(): jnp.einsum('ecf,efd->ecd', from_left, lax.dynamic_slice_in_dim(w_down, (i...  8.19 us
  transfers between devices with their start and end apart: 9, of which 6 were waited for; matrix products, arithmetic and copies ran while one was open for 11% of the time, Pallas kernels for 0%

profile of v1, /device:TPU:0, one launch (start us, length us, event | category | flops | bytes accessed | tf_op | source)
XLA Modules:
  0.0 174.3 jit_solution(17121791736678623432)
XLA Ops:
  6.5 8.7 %all_gather.26 = bf16[128,896]{1,0:T(8,128)(2,1)} all-gather(bf16[32,896]{1,0:T(8,128)(2,1)} %param.8), channel_id=1, replica_groups=mesh['expert'=4,'tensor'=8] {'expert'}, dimensions={0}, use_global_device_ids=true | all-gather | bytes 286720 | tf_op jit(solution)/shard_map/all_gather | solution.py:42
  15.5 1.2 dynamic-slice
  17.3 0.8 convert_reduce_fusion
  18.3 4.3 %all-reduce = s32[64]{0:T(128)S(1)} all-reduce(s32[64]{0:T(128)S(1)} %dynamic-update-slice), channel_id=2, replica_groups=mesh['expert'=4,'tensor'=8] {'expert'}, use_global_device_ids=true, to_apply=%add | all-reduce | flops 64 | bytes 512
  23.1 0.7 select_reduce_fusion.1
  23.8 5.2 %all-gather.2 = s32[4,32,8]{1,2,0:T(8,128)S(1)} all-gather(s32[1,32,8]{1,2,0:T(8,128)S(1)} %bitcast.35), channel_id=1, replica_groups=mesh['expert'=4,'tensor'=8] {'expert'}, dimensions={0}, use_global_device_ids=true | all-gather | bytes 5120 | tf_op jit(solution)/shard_map/all_gather | solution.py:39
  29.0 5.3 %all-gather.1 = s32[4,32,8]{1,2,0:T(8,128)S(1)} all-gather(s32[1,32,8]{1,2,0:T(8,128)} %bitcast.34), channel_id=1, replica_groups=mesh['expert'=4,'tensor'=8] {'expert'}, dimensions={0}, use_global_device_ids=true | all-gather | bytes 5120 | tf_op jit(solution)/shard_map/all_gather | solution.py:38
  34.4 5.3 %all-gather.3 = bf16[4,32,8]{1,2,0:T(8,128)(2,1)S(1)} all-gather(bf16[1,32,8]{1,2,0:T(8,128)(2,1)} %bitcast.36), channel_id=1, replica_groups=mesh['expert'=4,'tensor'=8] {'expert'}, dimensions={0}, use_global_device_ids=true | all-gather | bytes 2560 | tf_op jit(solution)/shard_map/all_gather | solution.py:43
  39.9 0.7 fusion
  41.3 21.1 %all-gather.6.cloned.1.call-done = bf16[128,7168]{1,0:T(8,128)(2,1)} async-done(((bf16[128,896]{1,0:T(8,128)(2,1)}), bf16[128,7168]{1,0:T(8,128)(2,1)}) %all-gather.6.cloned.1.call-update) | async-done | bytes 1835024 | tf_op jit(solution)/shard_map/all_gather | solution.py:45
  62.3 6.6 %convolution_convert_fusion = bf16[512,7168]{1,0:T(8,128)(2,1)} fusion(pred[128,512]{1,0:T(8,128)(4,1)S(1)} %fusion, bf16[128,7168]{1,0:T(8,128)(2,1)} %all-gather.6.cloned.1.call-done), kind=kOutput, calls=%fused_computation.2 | convolution fusion | flops 943194112 | bytes 9240576 | tf_op jit(solution)/shard_map/dot_general | solution.py:53
  68.9 12.3 %fusion.28 = f32[4,128,256]{2,1,0:T(8,128)S(1)} fusion(bf16[4,128,7168]{2,1,0:T(8,128)(2,1)} %bitcast.28, bf16[4,256,7168]{2,1,0:T(8,128)(2,1)} %param.11), kind=kOutput, calls=%fused_computation.39 | convolution fusion | flops 1879048192 | bytes 22544384 | tf_op jit(solution)/shard_map/ecd,efd->ecf/dot_general | solution.py:57
  81.2 12.3 %fusion.19 = bf16[4,128,256]{2,1,0:T(8,128)(2,1)S(1)} fusion(bf16[4,128,7168]{2,1,0:T(8,128)(2,1)} %bitcast.29, bf16[4,256,7168]{2,1,0:T(8,128)(2,1)} %param.12, f32[4,128,256]{2,1,0:T(8,128)S(1)} %fusion.28), kind=kOutput, calls=%fused_computation.24 | convolution fusion | flops 1879834624 | bytes 22806528 | tf_op jit(solution)/shard_map/ecd,efd->ecf/dot_general | solution.py:58
  93.5 2.2 %collective-permute-start = (bf16[4,128,256]{2,1,0:T(8,128)(2,1)S(1)}, bf16[4,128,256]{2,1,0:T(8,128)(2,1)S(1)}, u32[]{:S(2)}, u32[]{:S(2)}) collective-permute-start(bf16[4,128,256]{2,1,0:T(8,128)(2,1)S(1)} %fusion.19), channel_id=1, source_target_pairs={{0,7},{1,0},{2,1},{3,2},{4,3},{5,4},{6,5},{7,6},{8,15},{9,8},{10,9... | collective-permute-start | bytes 786440 | tf_op jit(solution)/shard_map/ppermute | solution.py:74
  95.7 2.0 %fusion.15 = f32[4,128,896]{2,1,0:T(8,128)S(1)} fusion(bf16[4,128,256]{2,1,0:T(8,128)(2,1)S(1)} %fusion.19, bf16[4,2048,896]{2,1,0:T(8,128)(2,1)} %param.13, s32[]{:T(128)S(6)} %select_n.91), kind=kOutput, calls=%fused_computation.21 | convolution fusion | flops 234881024 | bytes 3932164 | tf_op jit(solution)/shard_map/ecf,efd->ecd/dot_general | solution.py:65
  97.6 8.3 %collective-permute-done = bf16[4,128,256]{2,1,0:T(8,128)(2,1)S(1)} collective-permute-done((bf16[4,128,256]{2,1,0:T(8,128)(2,1)S(1)}, bf16[4,128,256]{2,1,0:T(8,128)(2,1)S(1)}, u32[]{:S(2)}, u32[]{:S(2)}) %collective-permute-start) | collective-permute-done | bytes 262176 | tf_op jit(solution)/shard_map/ppermute | solution.py:74
  105.9 2.0 %collective-permute-start.2 = (bf16[4,128,256]{2,1,0:T(8,128)(2,1)S(1)}, bf16[4,128,256]{2,1,0:T(8,128)(2,1)S(1)}, u32[]{:S(2)}, u32[]{:S(2)}) collective-permute-start(bf16[4,128,256]{2,1,0:T(8,128)(2,1)S(1)} %collective-permute-done), channel_id=1, source_target_pairs={{0,7},{1,0},{2,1},{3,2},{4,3},{5,4},{6,5},{7,6},{8,15},{9,8},{10,9... | collective-permute-start | bytes 786440 | tf_op jit(solution)/shard_map/ppermute | solution.py:74
  108.2 1.9 %fusion.11 = f32[4,128,896]{2,1,0:T(8,128)S(1)} fusion(bf16[4,128,256]{2,1,0:T(8,128)(2,1)S(1)} %collective-permute-done.1, bf16[4,2048,896]{2,1,0:T(8,128)(2,1)} %param.13, s32[]{:T(128)S(6)} %select_n.95), kind=kOutput, calls=%fused_computation.17 | convolution fusion | flops 234881024 | bytes 3932164 | tf_op jit(solution)/shard_map/ecf,efd->ecd/dot_general | solution.py:83
  110.2 2.0 %fusion.13 = f32[4,128,896]{2,1,0:T(8,128)S(1)} fusion(bf16[4,128,256]{2,1,0:T(8,128)(2,1)S(1)} %collective-permute-done, bf16[4,2048,896]{2,1,0:T(8,128)(2,1)} %param.13, s32[]{:T(128)S(6)} %select_n.93), kind=kOutput, calls=%fused_computation.19 | convolution fusion | flops 234881024 | bytes 3932164 | tf_op jit(solution)/shard_map/ecf,efd->ecd/dot_general | solution.py:75
  112.1 6.4 %collective-permute-done.2 = bf16[4,128,256]{2,1,0:T(8,128)(2,1)S(1)} collective-permute-done((bf16[4,128,256]{2,1,0:T(8,128)(2,1)S(1)}, bf16[4,128,256]{2,1,0:T(8,128)(2,1)S(1)}, u32[]{:S(2)}, u32[]{:S(2)}) %collective-permute-start.2) | collective-permute-done | bytes 262176 | tf_op jit(solution)/shard_map/ppermute | solution.py:74
  118.6 1.8 %collective-permute-start.4 = (bf16[4,128,256]{2,1,0:T(8,128)(2,1)S(1)}, bf16[4,128,256]{2,1,0:T(8,128)(2,1)S(1)}, u32[]{:S(2)}, u32[]{:S(2)}) collective-permute-start(bf16[4,128,256]{2,1,0:T(8,128)(2,1)S(1)} %collective-permute-done.2), channel_id=1, source_target_pairs={{0,7},{1,0},{2,1},{3,2},{4,3},{5,4},{6,5},{7,6},{8,15},{9,8},{10,9... | collective-permute-start | bytes 786440 | tf_op jit(solution)/shard_map/ppermute | solution.py:74
  120.9 2.0 %fusion.7 = f32[4,128,896]{2,1,0:T(8,128)S(1)} fusion(bf16[4,128,256]{2,1,0:T(8,128)(2,1)S(1)} %collective-permute-done.3, bf16[4,2048,896]{2,1,0:T(8,128)(2,1)} %param.13, s32[]{:T(128)S(6)} %select_n.99), kind=kOutput, calls=%fused_computation.13 | convolution fusion | flops 234881024 | bytes 3932164 | tf_op jit(solution)/shard_map/ecf,efd->ecd/dot_general | solution.py:83
  122.9 2.0 %fusion.9 = f32[4,128,896]{2,1,0:T(8,128)S(1)} fusion(bf16[4,128,256]{2,1,0:T(8,128)(2,1)S(1)} %collective-permute-done.2, bf16[4,2048,896]{2,1,0:T(8,128)(2,1)} %param.13, s32[]{:T(128)S(6)} %select_n.97), kind=kOutput, calls=%fused_computation.15 | convolution fusion | flops 234881024 | bytes 3932164 | tf_op jit(solution)/shard_map/ecf,efd->ecd/dot_general | solution.py:75
  124.8 6.4 %collective-permute-done.5 = bf16[4,128,256]{2,1,0:T(8,128)(2,1)S(1)} collective-permute-done((bf16[4,128,256]{2,1,0:T(8,128)(2,1)S(1)}, bf16[4,128,256]{2,1,0:T(8,128)(2,1)S(1)}, u32[]{:S(2)}, u32[]{:S(2)}) %collective-permute-start.5) | collective-permute-done | bytes 262176 | tf_op jit(solution)/shard_map/ppermute | solution.py:72
  131.2 2.5 %collective-permute-start.6 = (bf16[4,128,256]{2,1,0:T(8,128)(2,1)S(1)}, bf16[4,128,256]{2,1,0:T(8,128)(2,1)S(1)}, u32[]{:S(2)}, u32[]{:S(2)}) collective-permute-start(bf16[4,128,256]{2,1,0:T(8,128)(2,1)S(1)} %collective-permute-done.5), channel_id=1, source_target_pairs={{0,1},{1,2},{2,3},{3,4},{4,5},{5,6},{6,7},{7,0},{8,9},{9,10},{10,1... | collective-permute-start | bytes 786440 | tf_op jit(solution)/shard_map/ppermute | solution.py:72
  133.7 1.9 %fusion.3 = f32[4,128,896]{2,1,0:T(8,128)S(1)} fusion(bf16[4,128,256]{2,1,0:T(8,128)(2,1)S(1)} %collective-permute-done.5, bf16[4,2048,896]{2,1,0:T(8,128)(2,1)} %param.13, s32[]{:T(128)S(6)} %select_n.103), kind=kOutput, calls=%fused_computation.9 | convolution fusion | flops 234881024 | bytes 3932164 | tf_op jit(solution)/shard_map/ecf,efd->ecd/dot_general | solution.py:83
  135.7 2.0 %fusion.5 = f32[4,128,896]{2,1,0:T(8,128)S(1)} fusion(bf16[4,128,256]{2,1,0:T(8,128)(2,1)S(1)} %collective-permute-done.4, bf16[4,2048,896]{2,1,0:T(8,128)(2,1)} %param.13, s32[]{:T(128)S(6)} %select_n.101), kind=kOutput, calls=%fused_computation.11 | convolution fusion | flops 234881024 | bytes 3932164 | tf_op jit(solution)/shard_map/ecf,efd->ecd/dot_general | solution.py:75
  137.6 4.5 %collective-permute-done.6 = bf16[4,128,256]{2,1,0:T(8,128)(2,1)S(1)} collective-permute-done((bf16[4,128,256]{2,1,0:T(8,128)(2,1)S(1)}, bf16[4,128,256]{2,1,0:T(8,128)(2,1)S(1)}, u32[]{:S(2)}, u32[]{:S(2)}) %collective-permute-start.6) | collective-permute-done | bytes 262176 | tf_op jit(solution)/shard_map/ppermute | solution.py:72
  142.2 2.4 %add_add_fusion = f32[4,128,896]{2,1,0:T(8,128)S(1)} fusion(f32[4,128,896]{2,1,0:T(8,128)S(1)} %fusion.3, f32[4,128,896]{2,1,0:T(8,128)S(1)} %fusion.5, f32[4,128,896]{2,1,0:T(8,128)S(1)} %fusion.7, f32[4,128,896]{2,1,0:T(8,128)S(1)} %fusion.9, f32[4,128,896]{2,1,0:T(8,128)S(1)} %fusion.11, f32[4,128,896]{2,1,0:T(8,128)S(1)} %fusion.15, ...), kind=kOutput, calls=%fused_computation.8 | convolution fusion | flops 238092288 | bytes 16777220 | tf_op jit(solution)/shard_map/ecf,efd->ecd/dot_general | solution.py:83
  144.5 2.0 %fusion.29 = f32[128,896]{1,0:T(8,128)} fusion(f32[128,512]{1,0:T(8,128)S(1)} %select_reduce_fusion, f32[512,896]{1,0:T(8,128)S(1)} %bitcast.30), kind=kOutput, calls=%fused_computation.40 | convolution fusion | flops 704643072 | bytes 2555904 | tf_op jit(solution)/shard_map/dot_general | solution.py:93
  146.5 19.4 %reduce-scatter.2.cloned.1.call-done = f32[32,896]{1,0:T(8,128)} async-done(((f32[128,896]{1,0:T(8,128)}), f32[32,896]{1,0:T(8,128)}) %reduce-scatter.2.cloned.1.call-update) | async-done | bytes 114704 | tf_op jit(solution)/shard_map/reduce_scatter | solution.py:94
  165.9 1.5 convert_element_type.20
  (27 shorter events, 2.5 us)
Async XLA Ops:
  6.5 55.8 %all-gather.6.cloned.1.call-start = ((), (), s32[]{:S(2)}) async-start(), calls=%async_computation.1 | async-start | bytes 2064384 | tf_op jit(solution)/shard_map/all_gather | solution.py:45
  15.3 150.6 %reduce-scatter.2.cloned.1.call-start = ((), (), s32[]{:S(2)}) async-start(), calls=%async_computation.2 | async-start | bytes 573440 | tf_op jit(solution)/shard_map/reduce_scatter | solution.py:94
  93.5 12.4 %collective-permute-start = (bf16[4,128,256]{2,1,0:T(8,128)(2,1)S(1)}, bf16[4,128,256]{2,1,0:T(8,128)(2,1)S(1)}, u32[]{:S(2)}, u32[]{:S(2)}) collective-permute-start(bf16[4,128,256]{2,1,0:T(8,128)(2,1)S(1)} %fusion.19), channel_id=1, source_target_pairs={{0,7},{1,0},{2,1},{3,2},{4,3},{5,4},{6,5},{7,6},{8,15},{9,8},{10,9... | collective-permute-start | bytes 786440 | tf_op jit(solution)/shard_map/ppermute | solution.py:74
  95.7 12.3 %collective-permute-start.1 = (bf16[4,128,256]{2,1,0:T(8,128)(2,1)S(1)}, bf16[4,128,256]{2,1,0:T(8,128)(2,1)S(1)}, u32[]{:S(2)}, u32[]{:S(2)}) collective-permute-start(bf16[4,128,256]{2,1,0:T(8,128)(2,1)S(1)} %fusion.19), channel_id=1, source_target_pairs={{0,1},{1,2},{2,3},{3,4},{4,5},{5,6},{6,7},{7,0},{8,9},{9,10},{10,1... | collective-permute-start | bytes 786440 | tf_op jit(solution)/shard_map/ppermute | solution.py:72
  105.9 12.6 %collective-permute-start.2 = (bf16[4,128,256]{2,1,0:T(8,128)(2,1)S(1)}, bf16[4,128,256]{2,1,0:T(8,128)(2,1)S(1)}, u32[]{:S(2)}, u32[]{:S(2)}) collective-permute-start(bf16[4,128,256]{2,1,0:T(8,128)(2,1)S(1)} %collective-permute-done), channel_id=1, source_target_pairs={{0,7},{1,0},{2,1},{3,2},{4,3},{5,4},{6,5},{7,6},{8,15},{9,8},{10,9... | collective-permute-start | bytes 786440 | tf_op jit(solution)/shard_map/ppermute | solution.py:74
  107.9 12.4 %collective-permute-start.3 = (bf16[4,128,256]{2,1,0:T(8,128)(2,1)S(1)}, bf16[4,128,256]{2,1,0:T(8,128)(2,1)S(1)}, u32[]{:S(2)}, u32[]{:S(2)}) collective-permute-start(bf16[4,128,256]{2,1,0:T(8,128)(2,1)S(1)} %collective-permute-done.1), channel_id=1, source_target_pairs={{0,1},{1,2},{2,3},{3,4},{4,5},{5,6},{6,7},{7,0},{8,9},{9,10},{10,1... | collective-permute-start | bytes 786440 | tf_op jit(solution)/shard_map/ppermute | solution.py:72
  118.6 17.1 %collective-permute-start.4 = (bf16[4,128,256]{2,1,0:T(8,128)(2,1)S(1)}, bf16[4,128,256]{2,1,0:T(8,128)(2,1)S(1)}, u32[]{:S(2)}, u32[]{:S(2)}) collective-permute-start(bf16[4,128,256]{2,1,0:T(8,128)(2,1)S(1)} %collective-permute-done.2), channel_id=1, source_target_pairs={{0,7},{1,0},{2,1},{3,2},{4,3},{5,4},{6,5},{7,6},{8,15},{9,8},{10,9... | collective-permute-start | bytes 786440 | tf_op jit(solution)/shard_map/ppermute | solution.py:74
  120.3 10.9 %collective-permute-start.5 = (bf16[4,128,256]{2,1,0:T(8,128)(2,1)S(1)}, bf16[4,128,256]{2,1,0:T(8,128)(2,1)S(1)}, u32[]{:S(2)}, u32[]{:S(2)}) collective-permute-start(bf16[4,128,256]{2,1,0:T(8,128)(2,1)S(1)} %collective-permute-done.3), channel_id=1, source_target_pairs={{0,1},{1,2},{2,3},{3,4},{4,5},{5,6},{6,7},{7,0},{8,9},{9,10},{10,1... | collective-permute-start | bytes 786440 | tf_op jit(solution)/shard_map/ppermute | solution.py:72
  131.2 10.9 %collective-permute-start.6 = (bf16[4,128,256]{2,1,0:T(8,128)(2,1)S(1)}, bf16[4,128,256]{2,1,0:T(8,128)(2,1)S(1)}, u32[]{:S(2)}, u32[]{:S(2)}) collective-permute-start(bf16[4,128,256]{2,1,0:T(8,128)(2,1)S(1)} %collective-permute-done.5), channel_id=1, source_target_pairs={{0,1},{1,2},{2,3},{3,4},{4,5},{5,6},{6,7},{7,0},{8,9},{9,10},{10,1... | collective-permute-start | bytes 786440 | tf_op jit(solution)/shard_map/ppermute | solution.py:72
Sparse Core Ops, SparseCore 0:
  15.4 46.8 all-gather.5
  146.7 19.1 reduce-scatter.1
